TPU v7x, 32 devices: a whole 2x2x4 slice. The times are simulated.
32 devices in a mesh: dp: 8 (over z, core), ctx: 4 (over y, x).
Axes of the slice: x: 2, y: 2, z: 4, core: 2. Of those that a mesh axis runs over, the one named last changes fastest.
Arguments:
- state_rows: bfloat16 [12288, 2048], P(('dp', 'ctx')), parts along dimension 0, may hold values from -6 to 6
- query_vectors: bfloat16 [8, 12288, 128], P(None, ('dp', 'ctx')), parts along dimension 1, may hold values from -6 to 6
- key_vectors: bfloat16 [8, 12288, 128], P(None, ('dp', 'ctx')), parts along dimension 1, may hold values from -6 to 6
- value_vectors: bfloat16 [8, 12288, 128], P(None, ('dp', 'ctx')), parts along dimension 1, may hold values from -24 to 24
- halt_counts: int32 [12288], P(('dp', 'ctx')), parts along dimension 0, may hold values from 1 to 6, as said below
- out_weight: bfloat16 [8, 128, 2048], replicated, may hold values from -0.75 to 0.75
- norm_gain: bfloat16 [2048], replicated, may hold values from 0.099609375 to 1.8984375
Outputs:
- new_state: bfloat16 [12288, 2048], P(('dp', 'ctx')), parts along dimension 0
There are 8 independent parts, one for each index of `dp`. A program takes and returns all parts, laid end to end along the dimension named above; an argument that names none is the same for every part. Nothing has to cross between parts.
Inputs may be any that keep to these rules, and one draw needn't show every extreme that they name: halt_counts is equal within each aligned tile of 128 positions; exactly 3 tiles of a document have counts above 2, and on some device of ctx all 3 tiles do.
All inputs are finite; a program needn't handle non-finite values.
Results may differ from a plain program's by a relative error of at most 0.008.
Values may be sent and summed in bfloat16 or wider, within the bound.
A program may use at most 128 MiB of HBM per device.

v0:
```python
import jax
import jax.numpy as jnp
from jax import lax
from jax.sharding import PartitionSpec as P

STEP = 2


def fold_heads(carry, queries, key_piece, value_piece, score_scale):
    running_max, running_sum, weighted = carry

    def per_head(head_items):
        query_head, key_head, value_head, max_head, sum_head, weighted_head = head_items
        scores = (
            lax.dot_general(
                query_head, key_head, (((1,), (1,)), ((), ())), preferred_element_type=jnp.float32
            )
            * score_scale
        )
        new_max = jnp.maximum(max_head, jnp.max(scores, axis=1))
        shrink = jnp.exp(max_head - new_max)
        exponents = jnp.exp(scores - new_max[:, None])
        sum_head = sum_head * shrink + jnp.sum(exponents, axis=1)
        weighted_head = weighted_head * shrink[:, None] + jnp.dot(
            exponents.astype(jnp.bfloat16), value_head, preferred_element_type=jnp.float32
        )
        return (new_max, sum_head, weighted_head)

    return lax.map(per_head, (queries, key_piece, value_piece, running_max, running_sum, weighted))


def empty_carry(head_count, query_count, head_width):
    return (
        jnp.full((head_count, query_count), -1e30, jnp.float32),
        jnp.zeros((head_count, query_count), jnp.float32),
        jnp.zeros((head_count, query_count, head_width), jnp.float32),
    )


def attend_keys(query_vectors, key_vectors, value_vectors, score_scale):
    head_count, row_count, head_width = query_vectors.shape
    initial = empty_carry(head_count, row_count, head_width)
    running_max, running_sum, weighted = fold_heads(
        initial,
        query_vectors,
        lax.all_gather(key_vectors, "ctx", axis=1, tiled=True),
        lax.all_gather(value_vectors, "ctx", axis=1, tiled=True),
        score_scale,
    )
    return (weighted / running_sum[..., None]).astype(jnp.bfloat16)


def on_device(
    state_rows, query_vectors, key_vectors, value_vectors, halt_counts, out_weight, norm_gain
):
    head_count, row_count, head_width = query_vectors.shape
    score_scale = head_width ** (-0.5)
    attended = attend_keys(query_vectors, key_vectors, value_vectors, score_scale)
    update = jnp.einsum("hqd,hde->qe", attended, out_weight, preferred_element_type=jnp.float32)
    mixed_sum = state_rows.astype(jnp.float32) + update
    normed = (
        mixed_sum
        * lax.rsqrt(jnp.mean(mixed_sum * mixed_sum, axis=-1, keepdims=True) + 1e-06)
        * norm_gain.astype(jnp.float32)
    )
    active = (halt_counts > STEP)[:, None]
    return jnp.where(active, normed.astype(jnp.bfloat16), state_rows)


def solution(mesh):
    placed = (
        P(("dp", "ctx"), None),
        P(None, ("dp", "ctx"), None),
        P(None, ("dp", "ctx"), None),
        P(None, ("dp", "ctx"), None),
        P(("dp", "ctx")),
        P(),
        P(),
    )
    return jax.shard_map(
        on_device, mesh=mesh, in_specs=placed, out_specs=P(("dp", "ctx"), None), check_vma=False
    )
```

profile of v0, /device:TPU:0, one launch (start us, length us, event | category | flops | bytes accessed | tf_op | source)
XLA Modules:
  0.0 150.3 jit_solution(8866256472894087559)
XLA Ops:
  6.5 0.0 all-gather.3.cloned.1.call-start
  6.5 0.7 all-gather.3.cloned.1.call-update
  7.3 0.0 all-gather.5.cloned.1.call-start
  7.3 0.7 all-gather.5.cloned.1.call-update
  8.0 0.7 convert_element_type.17
  8.7 0.7 broadcast_compare_fusion
  9.4 46.4 %all-gather.3.cloned.1.call-done = bf16[8,1536,128]{2,1,0:T(8,128)(2,1)} async-done(((bf16[8,384,128]{2,1,0:T(8,128)(2,1)}), bf16[8,1536,128]{2,1,0:T(8,128)(2,1)}) %all-gather.3.cloned.1.call-update) | async-done | bytes 3145744 | tf_op jit(solution)/shard_map/all_gather | solution.py:46
  55.8 45.7 %all-gather.5.cloned.1.call-done = bf16[8,1536,128]{2,1,0:T(8,128)(2,1)} async-done(((bf16[8,384,128]{2,1,0:T(8,128)(2,1)}), bf16[8,1536,128]{2,1,0:T(8,128)(2,1)}) %all-gather.5.cloned.1.call-update) | async-done | bytes 3145744 | tf_op jit(solution)/shard_map/all_gather | solution.py:47
  101.5 35.0 %while.12 = (s32[]{:T(128)}, f32[8,384]{1,0:T(8,128)S(1)}, f32[8,384,128]{2,1,0:T(8,128)}, bf16[8,384,128]{2,1,0:T(8,128)(2,1)}, bf16[8,1536,128]{2,1,0:T(8,128)...) while((s32[]{:T(128)}, f32[8,384]{1,0:T(8,128)S(1)}, f32[8,384,128]{2,1,0:T(8,128)}, ...), condition=%wide.region_3.4_spmd, body=%wide.region_0.3_spmd.sunk | while | flops 305579136 | bytes 8184417 | solution.py:29
  101.5 1.6 %fusion.34 = (f32[384]{0:T(512)S(1)}, f32[384,1536]{1,0:T(8,128)S(1)}) fusion(bf16[8,1536,128]{2,1,0:T(8,128)(2,1)} %get-tuple-element.123, s32[]{:T(128)S(6)} %copy.13, bf16[8,384,128]{2,1,0:T(8,128)(2,1)} %get-tuple-element.122), kind=kOutput, calls=%fused_computation.28.clone.1 | convolution fusion | flops 152174208 | bytes 2853376 | tf_op jit(solution)/shard_map/while/body/eval_jaxpr/dot_general | solution.py:15
  103.1 0.5 fusion.35
  103.6 0.1 dynamic_update_slice.12
  103.7 2.2 %fusion.36 = f32[8,384,128]{2,1,0:T(8,128)} fusion(f32[8,384,128]{2,1,0:T(8,128)} %get-tuple-element.113, s32[]{:T(128)S(6)} %copy.13, f32[384,1536]{1,0:T(8,128)S(1)} %get-tuple-element.100, f32[384]{0:T(512)S(1)} %broadcast_maximum_fusion.2, bf16[8,1536,128]{2,1,0:T(8,128)(2,1)} %get-tuple-element.124, f32[384]{0:T(512)S(1)} %get-tuple-element.102), kind=kOutput, calls=%fused_computation.8.clone.1 | convolution fusion | flops 152223744 | bytes 2953216 | tf_op jit(solution)/shard_map/while/body/eval_jaxpr/dot_general | solution.py:24
  105.9 1.6 %fusion.34 = (f32[384]{0:T(512)S(1)}, f32[384,1536]{1,0:T(8,128)S(1)}) fusion(bf16[8,1536,128]{2,1,0:T(8,128)(2,1)} %get-tuple-element.123, s32[]{:T(128)S(6)} %copy.13, bf16[8,384,128]{2,1,0:T(8,128)(2,1)} %get-tuple-element.122), kind=kOutput, calls=%fused_computation.28.clone.1 | convolution fusion | flops 152174208 | bytes 2853376 | tf_op jit(solution)/shard_map/while/body/eval_jaxpr/dot_general | solution.py:15
  107.5 0.5 fusion.35
  108.0 0.1 dynamic_update_slice.12
  108.0 2.2 %fusion.36 = f32[8,384,128]{2,1,0:T(8,128)} fusion(f32[8,384,128]{2,1,0:T(8,128)} %get-tuple-element.113, s32[]{:T(128)S(6)} %copy.13, f32[384,1536]{1,0:T(8,128)S(1)} %get-tuple-element.100, f32[384]{0:T(512)S(1)} %broadcast_maximum_fusion.2, bf16[8,1536,128]{2,1,0:T(8,128)(2,1)} %get-tuple-element.124, f32[384]{0:T(512)S(1)} %get-tuple-element.102), kind=kOutput, calls=%fused_computation.8.clone.1 | convolution fusion | flops 152223744 | bytes 2953216 | tf_op jit(solution)/shard_map/while/body/eval_jaxpr/dot_general | solution.py:24
  110.2 1.6 %fusion.34 = (f32[384]{0:T(512)S(1)}, f32[384,1536]{1,0:T(8,128)S(1)}) fusion(bf16[8,1536,128]{2,1,0:T(8,128)(2,1)} %get-tuple-element.123, s32[]{:T(128)S(6)} %copy.13, bf16[8,384,128]{2,1,0:T(8,128)(2,1)} %get-tuple-element.122), kind=kOutput, calls=%fused_computation.28.clone.1 | convolution fusion | flops 152174208 | bytes 2853376 | tf_op jit(solution)/shard_map/while/body/eval_jaxpr/dot_general | solution.py:15
  111.9 0.5 fusion.35
  112.4 0.1 dynamic_update_slice.12
  112.4 2.2 %fusion.36 = f32[8,384,128]{2,1,0:T(8,128)} fusion(f32[8,384,128]{2,1,0:T(8,128)} %get-tuple-element.113, s32[]{:T(128)S(6)} %copy.13, f32[384,1536]{1,0:T(8,128)S(1)} %get-tuple-element.100, f32[384]{0:T(512)S(1)} %broadcast_maximum_fusion.2, bf16[8,1536,128]{2,1,0:T(8,128)(2,1)} %get-tuple-element.124, f32[384]{0:T(512)S(1)} %get-tuple-element.102), kind=kOutput, calls=%fused_computation.8.clone.1 | convolution fusion | flops 152223744 | bytes 2953216 | tf_op jit(solution)/shard_map/while/body/eval_jaxpr/dot_general | solution.py:24
  114.6 1.6 %fusion.34 = (f32[384]{0:T(512)S(1)}, f32[384,1536]{1,0:T(8,128)S(1)}) fusion(bf16[8,1536,128]{2,1,0:T(8,128)(2,1)} %get-tuple-element.123, s32[]{:T(128)S(6)} %copy.13, bf16[8,384,128]{2,1,0:T(8,128)(2,1)} %get-tuple-element.122), kind=kOutput, calls=%fused_computation.28.clone.1 | convolution fusion | flops 152174208 | bytes 2853376 | tf_op jit(solution)/shard_map/while/body/eval_jaxpr/dot_general | solution.py:15
  116.2 0.5 fusion.35
  116.7 0.1 dynamic_update_slice.12
  116.8 2.2 %fusion.36 = f32[8,384,128]{2,1,0:T(8,128)} fusion(f32[8,384,128]{2,1,0:T(8,128)} %get-tuple-element.113, s32[]{:T(128)S(6)} %copy.13, f32[384,1536]{1,0:T(8,128)S(1)} %get-tuple-element.100, f32[384]{0:T(512)S(1)} %broadcast_maximum_fusion.2, bf16[8,1536,128]{2,1,0:T(8,128)(2,1)} %get-tuple-element.124, f32[384]{0:T(512)S(1)} %get-tuple-element.102), kind=kOutput, calls=%fused_computation.8.clone.1 | convolution fusion | flops 152223744 | bytes 2953216 | tf_op jit(solution)/shard_map/while/body/eval_jaxpr/dot_general | solution.py:24
  119.0 1.6 %fusion.34 = (f32[384]{0:T(512)S(1)}, f32[384,1536]{1,0:T(8,128)S(1)}) fusion(bf16[8,1536,128]{2,1,0:T(8,128)(2,1)} %get-tuple-element.123, s32[]{:T(128)S(6)} %copy.13, bf16[8,384,128]{2,1,0:T(8,128)(2,1)} %get-tuple-element.122), kind=kOutput, calls=%fused_computation.28.clone.1 | convolution fusion | flops 152174208 | bytes 2853376 | tf_op jit(solution)/shard_map/while/body/eval_jaxpr/dot_general | solution.py:15
  120.6 0.5 fusion.35
  121.1 0.1 dynamic_update_slice.12
  121.2 2.2 %fusion.36 = f32[8,384,128]{2,1,0:T(8,128)} fusion(f32[8,384,128]{2,1,0:T(8,128)} %get-tuple-element.113, s32[]{:T(128)S(6)} %copy.13, f32[384,1536]{1,0:T(8,128)S(1)} %get-tuple-element.100, f32[384]{0:T(512)S(1)} %broadcast_maximum_fusion.2, bf16[8,1536,128]{2,1,0:T(8,128)(2,1)} %get-tuple-element.124, f32[384]{0:T(512)S(1)} %get-tuple-element.102), kind=kOutput, calls=%fused_computation.8.clone.1 | convolution fusion | flops 152223744 | bytes 2953216 | tf_op jit(solution)/shard_map/while/body/eval_jaxpr/dot_general | solution.py:24
  123.4 1.6 %fusion.34 = (f32[384]{0:T(512)S(1)}, f32[384,1536]{1,0:T(8,128)S(1)}) fusion(bf16[8,1536,128]{2,1,0:T(8,128)(2,1)} %get-tuple-element.123, s32[]{:T(128)S(6)} %copy.13, bf16[8,384,128]{2,1,0:T(8,128)(2,1)} %get-tuple-element.122), kind=kOutput, calls=%fused_computation.28.clone.1 | convolution fusion | flops 152174208 | bytes 2853376 | tf_op jit(solution)/shard_map/while/body/eval_jaxpr/dot_general | solution.py:15
  125.0 0.5 fusion.35
  125.5 0.1 dynamic_update_slice.12
  125.5 2.2 %fusion.36 = f32[8,384,128]{2,1,0:T(8,128)} fusion(f32[8,384,128]{2,1,0:T(8,128)} %get-tuple-element.113, s32[]{:T(128)S(6)} %copy.13, f32[384,1536]{1,0:T(8,128)S(1)} %get-tuple-element.100, f32[384]{0:T(512)S(1)} %broadcast_maximum_fusion.2, bf16[8,1536,128]{2,1,0:T(8,128)(2,1)} %get-tuple-element.124, f32[384]{0:T(512)S(1)} %get-tuple-element.102), kind=kOutput, calls=%fused_computation.8.clone.1 | convolution fusion | flops 152223744 | bytes 2953216 | tf_op jit(solution)/shard_map/while/body/eval_jaxpr/dot_general | solution.py:24
  127.8 1.6 %fusion.34 = (f32[384]{0:T(512)S(1)}, f32[384,1536]{1,0:T(8,128)S(1)}) fusion(bf16[8,1536,128]{2,1,0:T(8,128)(2,1)} %get-tuple-element.123, s32[]{:T(128)S(6)} %copy.13, bf16[8,384,128]{2,1,0:T(8,128)(2,1)} %get-tuple-element.122), kind=kOutput, calls=%fused_computation.28.clone.1 | convolution fusion | flops 152174208 | bytes 2853376 | tf_op jit(solution)/shard_map/while/body/eval_jaxpr/dot_general | solution.py:15
  129.4 0.5 fusion.35
  129.9 0.1 dynamic_update_slice.12
  129.9 2.2 %fusion.36 = f32[8,384,128]{2,1,0:T(8,128)} fusion(f32[8,384,128]{2,1,0:T(8,128)} %get-tuple-element.113, s32[]{:T(128)S(6)} %copy.13, f32[384,1536]{1,0:T(8,128)S(1)} %get-tuple-element.100, f32[384]{0:T(512)S(1)} %broadcast_maximum_fusion.2, bf16[8,1536,128]{2,1,0:T(8,128)(2,1)} %get-tuple-element.124, f32[384]{0:T(512)S(1)} %get-tuple-element.102), kind=kOutput, calls=%fused_computation.8.clone.1 | convolution fusion | flops 152223744 | bytes 2953216 | tf_op jit(solution)/shard_map/while/body/eval_jaxpr/dot_general | solution.py:24
  132.1 1.6 %fusion.34 = (f32[384]{0:T(512)S(1)}, f32[384,1536]{1,0:T(8,128)S(1)}) fusion(bf16[8,1536,128]{2,1,0:T(8,128)(2,1)} %get-tuple-element.123, s32[]{:T(128)S(6)} %copy.13, bf16[8,384,128]{2,1,0:T(8,128)(2,1)} %get-tuple-element.122), kind=kOutput, calls=%fused_computation.28.clone.1 | convolution fusion | flops 152174208 | bytes 2853376 | tf_op jit(solution)/shard_map/while/body/eval_jaxpr/dot_general | solution.py:15
  133.8 0.5 fusion.35
  134.2 0.1 dynamic_update_slice.12
  134.3 2.2 %fusion.36 = f32[8,384,128]{2,1,0:T(8,128)} fusion(f32[8,384,128]{2,1,0:T(8,128)} %get-tuple-element.113, s32[]{:T(128)S(6)} %copy.13, f32[384,1536]{1,0:T(8,128)S(1)} %get-tuple-element.100, f32[384]{0:T(512)S(1)} %broadcast_maximum_fusion.2, bf16[8,1536,128]{2,1,0:T(8,128)(2,1)} %get-tuple-element.124, f32[384]{0:T(512)S(1)} %get-tuple-element.102), kind=kOutput, calls=%fused_computation.8.clone.1 | convolution fusion | flops 152223744 | bytes 2953216 | tf_op jit(solution)/shard_map/while/body/eval_jaxpr/dot_general | solution.py:24
  136.5 0.0 copy-start
  136.5 5.2 %multiply_reduce_fusion = (f32[384]{0:T(512)S(1)}, f32[384,2048]{1,0:T(8,128)S(1)}) fusion(bf16[8,128,2048]{2,1,0:T(8,128)(2,1)} %param.14, f32[8,384,128]{2,1,0:T(8,128)} %get-tuple-element.38, f32[8,384]{1,0:T(8,128)S(1)} %get-tuple-element.39, bf16[384,2048]{1,0:T(8,128)(2,1)} %param.9), kind=kOutput, calls=%fused_computation.22 | convolution fusion | flops 1614544512 | bytes 10499584 | tf_op jit(solution)/shard_map/hqd,hde->qe/dot_general | solution.py:59
  141.8 0.0 copy-done
  141.8 1.7 %fusion.23 = bf16[384,2048]{1,0:T(8,128)(2,1)} fusion(bf16[384,2048]{1,0:T(8,128)(2,1)S(1)} %copy-done, f32[384,2048]{1,0:T(8,128)S(1)} %get-tuple-element.57, f32[2048]{0:T(1024)S(1)} %convert_element_type.17, f32[384]{0:T(512)S(1)} %add_rsqrt_fusion, pred[384]{0:T(512)(128)(4,1)S(1)} %broadcast_compare_fusion), kind=kLoop, calls=%fused_computation.23 | loop fusion | flops 3145728 | bytes 6301568 | tf_op jit(solution)/shard_map/jit(_where)/select_n | solution.py:67
  (27 shorter events, 0.2 us)
Async XLA Ops:
  6.5 49.2 %all-gather.3.cloned.1.call-start = ((), (), s32[]{:S(2)}) async-start(), calls=%async_computation | async-start | bytes 3932160 | tf_op jit(solution)/shard_map/all_gather | solution.py:46
  7.3 94.2 %all-gather.5.cloned.1.call-start = ((), (), s32[]{:S(2)}) async-start(), calls=%async_computation.1 | async-start | bytes 3932160 | tf_op jit(solution)/shard_map/all_gather | solution.py:47
  136.5 5.2 %copy-start = (bf16[384,2048]{1,0:T(8,128)(2,1)S(1)}, bf16[384,2048]{1,0:T(8,128)(2,1)}, u32[]{:S(2)}) copy-start(bf16[384,2048]{1,0:T(8,128)(2,1)} %param.9) | copy-start | bytes 4718596
Sparse Core Ops, SparseCore 0:
  9.2 46.5 all-gather.2
  57.6 43.8 all-gather.4
where the time goes:
time: 151 us; the launch traced here: 150 us
  waiting for transfers between devices  93.5 us (62%)
  matrix products  35.8 us (24%)
  between operations  13.4 us (9%)
  other arithmetic  6.97 us (5%)
    all_gather x1, waiting for transfers between devices, attend_keys(): lax.all_gather(key_vectors, 'ctx', axis=1, tiled=True)  46.4 us
    all_gather x1, waiting for transfers between devices, attend_keys(): lax.all_gather(value_vectors, 'ctx', axis=1, tiled=True)  45.7 us
    dot_general x8, matrix products, per_head(): jnp.dot(exponents.astype(jnp.bfloat16), value_head, preferred_element_typ...  17.7 us
    dot_general x8, matrix products, per_head(): lax.dot_general(query_head, key_head, (((1,), (1,)), ((), ())), preferred...  12.8 us
    dot_general x1, matrix products, on_device(): jnp.einsum('hqd,hde->qe', attended, out_weight, preferred_element_type=jn...  5.22 us
    reduce_sum x8, other arithmetic, per_head(): sum_head = sum_head * shrink + jnp.sum(exponents, axis=1)  3.76 us
  transfers between devices with their start and end apart: 2, of which 2 were waited for; matrix products, arithmetic and copies ran while one was open for 1% of the time, Pallas kernels for 0%

commit v1 on v0

--- a/solution.py
+++ b/solution.py
@@ -43,7 +43,9 @@
     running_max, running_sum, weighted = fold_heads(
         initial,
         query_vectors,
-        lax.all_gather(key_vectors, "ctx", axis=1, tiled=True),
+        jnp.concatenate(
+            lax.all_to_all(jnp.stack([key_vectors] * lax.axis_size("ctx")), "ctx", 0, 0), axis=1
+        ),
         lax.all_gather(value_vectors, "ctx", axis=1, tiled=True),
         score_scale,
     )

time: 151 us -> 127 us (0.84)
  waiting for transfers between devices: 93.5 us -> 60.5 us
  local copies, waits for them, and re-layouts: 0.46 us -> 5.87 us
  starting transfers between devices: 0.04 us -> 5.33 us
    all_gather x1 -> x0, waiting for transfers between devices: 46.4 us -> none  [attend_keys(): lax.all_gather(key_vectors, 'ctx', axis=1, tiled=True)]
    all_to_all x0 -> x1, waiting for transfers between devices: none -> 45 us  [attend_keys(): lax.all_to_all(jnp.stack([key_vectors] * lax.axis_size('ctx')), 'ctx', 0, 0)]
    all_gather x1, waiting for transfers between devices: 45.7 us -> 14.8 us  [attend_keys(): lax.all_gather(value_vectors, 'ctx', axis=1, tiled=True)]
    all_to_all x0 -> x1, starting transfers between devices: none -> 5.32 us  [attend_keys(): lax.all_to_all(jnp.stack([key_vectors] * lax.axis_size('ctx')), 'ctx', 0, 0)]
    another operation x0 -> x1, local copies, waits for them, and re-layouts: none -> 3.53 us  [attend_keys(): jnp.stack([key_vectors] * lax.axis_size('ctx'))]
    all_to_all x0 -> x1, local copies, waits for them, and re-layouts: none -> 1.88 us  [attend_keys(): lax.all_to_all(jnp.stack([key_vectors] * lax.axis_size('ctx')), 'ctx', 0, 0)]
  transfers between devices with their start and end apart: 2 -> 2, of which waited for: 2 -> 2; matrix products, arithmetic and copies ran while one was open for 1% -> 4% of each run, Pallas kernels for 0% -> 0%
where the time goes in v1:
time: 127 us
  waiting for transfers between devices  60.5 us (48%)
  matrix products  35.7 us (28%)
  between operations  13.4 us (11%)
  local copies, waits for them, and re-layouts  5.87 us (5%)
  other arithmetic  5.59 us (4%)
  starting transfers between devices  5.33 us (4%)
    all_to_all x1, waiting for transfers between devices, attend_keys(): lax.all_to_all(jnp.stack([key_vectors] * lax.axis_size('ctx')), 'ctx', 0, 0)  45 us
    dot_general x8, matrix products, per_head(): jnp.dot(exponents.astype(jnp.bfloat16), value_head, preferred_element_typ...  17.7 us
    all_gather x1, waiting for transfers between devices, attend_keys(): lax.all_gather(value_vectors, 'ctx', axis=1, tiled=True)  14.8 us
    dot_general x8, matrix products, per_head(): lax.dot_general(query_head, key_head, (((1,), (1,)), ((), ())), preferred...  12.8 us
    all_to_all x1, starting transfers between devices, attend_keys(): lax.all_to_all(jnp.stack([key_vectors] * lax.axis_size('ctx')), 'ctx', 0, 0)  5.32 us
    dot_general x1, matrix products, on_device(): jnp.einsum('hqd,hde->qe', attended, out_weight, preferred_element_type=jn...  5.23 us
    reduce_sum x8, other arithmetic, per_head(): sum_head = sum_head * shrink + jnp.sum(exponents, axis=1)  3.75 us
    another operation x1, local copies, waits for them, and re-layouts, attend_keys(): jnp.stack([key_vectors] * lax.axis_size('ctx'))  3.53 us
  transfers between devices with their start and end apart: 2, of which 2 were waited for; matrix products, arithmetic and copies ran while one was open for 4% of the time, Pallas kernels for 0%

profile of v1, /device:TPU:0, one launch (start us, length us, event | category | flops | bytes accessed | tf_op | source)
XLA Modules:
  0.0 126.5 jit_solution(18171842207664107984)
XLA Ops:
  6.5 0.0 all-gather.2.cloned.1.call-start
  6.5 0.7 all-gather.2.cloned.1.call-update
  7.3 3.5 %stack.2 = bf16[4,8,384,128]{3,2,1,0:T(8,128)(2,1)} broadcast(bf16[8,384,128]{2,1,0:T(8,128)(2,1)} %param.11), dimensions={1,2,3} | broadcast | bytes 3932160 | tf_op jit(solution)/shard_map/stack | solution.py:47
  10.8 0.0 copy-start.1
  10.8 0.0 copy-start.2
  10.8 5.3 %all-to-all-start = ((bf16[4,8,384,128]{3,2,1,0:T(8,128)(2,1)}), bf16[4,8,384,128]{3,2,1,0:T(8,128)(2,1)S(1)}, u32[]{:S(2)}, u32[]{:S(2)}) async-start(bf16[4,8,384,128]{3,2,1,0:T(8,128)(2,1)} %stack.2), calls=%async_computation | async-start | bytes 6291456 | tf_op jit(solution)/shard_map/all_to_all | solution.py:47
  16.1 0.0 copy-done.1
  16.1 0.0 copy-done.2
  16.1 45.0 %all-to-all-done = bf16[4,8,384,128]{3,2,1,0:T(8,128)(2,1)S(1)} async-done(((bf16[4,8,384,128]{3,2,1,0:T(8,128)(2,1)}), bf16[4,8,384,128]{3,2,1,0:T(8,128)(2,1)S(1)}, u32[]{:S(2)}, u32[]{:S(2)}) %all-to-all-start) | async-done | bytes 3145760 | tf_op jit(solution)/shard_map/all_to_all | solution.py:47
  61.1 1.9 %copy.8 = bf16[4,8,384,128]{3,2,0,1:T(8,128)(2,1)} copy(bf16[4,8,384,128]{3,2,1,0:T(8,128)(2,1)S(1)} %all-to-all-done) | data formatting | bytes 6291456 | tf_op jit(solution)/shard_map/all_to_all | solution.py:47
  63.0 14.8 %all-gather.2.cloned.1.call-done = bf16[8,1536,128]{2,1,0:T(8,128)(2,1)} async-done(((bf16[8,384,128]{2,1,0:T(8,128)(2,1)}), bf16[8,1536,128]{2,1,0:T(8,128)(2,1)}) %all-gather.2.cloned.1.call-update) | async-done | bytes 3145744 | tf_op jit(solution)/shard_map/all_gather | solution.py:49
  77.8 35.0 %while.12 = (s32[]{:T(128)}, f32[8,384]{1,0:T(8,128)S(1)}, f32[8,384,128]{2,1,0:T(8,128)}, bf16[8,384,128]{2,1,0:T(8,128)(2,1)}, bf16[8,1536,128]{2,1,0:T(8,128)...) while((s32[]{:T(128)}, f32[8,384]{1,0:T(8,128)S(1)}, f32[8,384,128]{2,1,0:T(8,128)}, ...), condition=%wide.region_3.4_spmd, body=%wide.region_0.3_spmd.sunk | while | flops 305579136 | bytes 8184417 | solution.py:29
  77.8 1.6 %fusion.34 = (f32[384]{0:T(512)S(1)}, f32[384,1536]{1,0:T(8,128)S(1)}) fusion(bf16[8,1536,128]{2,1,0:T(8,128)(2,1)} %get-tuple-element.123, s32[]{:T(128)S(6)} %copy.14, bf16[8,384,128]{2,1,0:T(8,128)(2,1)} %get-tuple-element.122), kind=kOutput, calls=%fused_computation.28.clone.1 | convolution fusion | flops 152174208 | bytes 2853376 | tf_op jit(solution)/shard_map/while/body/eval_jaxpr/dot_general | solution.py:15
  79.4 0.5 fusion.35
  79.9 0.1 dynamic_update_slice.12
  79.9 2.2 %fusion.36 = f32[8,384,128]{2,1,0:T(8,128)} fusion(f32[8,384,128]{2,1,0:T(8,128)} %get-tuple-element.113, s32[]{:T(128)S(6)} %copy.14, f32[384,1536]{1,0:T(8,128)S(1)} %get-tuple-element.100, f32[384]{0:T(512)S(1)} %broadcast_maximum_fusion.2, bf16[8,1536,128]{2,1,0:T(8,128)(2,1)} %get-tuple-element.124, f32[384]{0:T(512)S(1)} %get-tuple-element.102), kind=kOutput, calls=%fused_computation.8.clone.1 | convolution fusion | flops 152223744 | bytes 2953216 | tf_op jit(solution)/shard_map/while/body/eval_jaxpr/dot_general | solution.py:24
  82.2 1.6 %fusion.34 = (f32[384]{0:T(512)S(1)}, f32[384,1536]{1,0:T(8,128)S(1)}) fusion(bf16[8,1536,128]{2,1,0:T(8,128)(2,1)} %get-tuple-element.123, s32[]{:T(128)S(6)} %copy.14, bf16[8,384,128]{2,1,0:T(8,128)(2,1)} %get-tuple-element.122), kind=kOutput, calls=%fused_computation.28.clone.1 | convolution fusion | flops 152174208 | bytes 2853376 | tf_op jit(solution)/shard_map/while/body/eval_jaxpr/dot_general | solution.py:15
  83.8 0.5 fusion.35
  84.3 0.1 dynamic_update_slice.12
  84.3 2.2 %fusion.36 = f32[8,384,128]{2,1,0:T(8,128)} fusion(f32[8,384,128]{2,1,0:T(8,128)} %get-tuple-element.113, s32[]{:T(128)S(6)} %copy.14, f32[384,1536]{1,0:T(8,128)S(1)} %get-tuple-element.100, f32[384]{0:T(512)S(1)} %broadcast_maximum_fusion.2, bf16[8,1536,128]{2,1,0:T(8,128)(2,1)} %get-tuple-element.124, f32[384]{0:T(512)S(1)} %get-tuple-element.102), kind=kOutput, calls=%fused_computation.8.clone.1 | convolution fusion | flops 152223744 | bytes 2953216 | tf_op jit(solution)/shard_map/while/body/eval_jaxpr/dot_general | solution.py:24
  86.5 1.6 %fusion.34 = (f32[384]{0:T(512)S(1)}, f32[384,1536]{1,0:T(8,128)S(1)}) fusion(bf16[8,1536,128]{2,1,0:T(8,128)(2,1)} %get-tuple-element.123, s32[]{:T(128)S(6)} %copy.14, bf16[8,384,128]{2,1,0:T(8,128)(2,1)} %get-tuple-element.122), kind=kOutput, calls=%fused_computation.28.clone.1 | convolution fusion | flops 152174208 | bytes 2853376 | tf_op jit(solution)/shard_map/while/body/eval_jaxpr/dot_general | solution.py:15
  88.1 0.5 fusion.35
  88.6 0.1 dynamic_update_slice.12
  88.7 2.2 %fusion.36 = f32[8,384,128]{2,1,0:T(8,128)} fusion(f32[8,384,128]{2,1,0:T(8,128)} %get-tuple-element.113, s32[]{:T(128)S(6)} %copy.14, f32[384,1536]{1,0:T(8,128)S(1)} %get-tuple-element.100, f32[384]{0:T(512)S(1)} %broadcast_maximum_fusion.2, bf16[8,1536,128]{2,1,0:T(8,128)(2,1)} %get-tuple-element.124, f32[384]{0:T(512)S(1)} %get-tuple-element.102), kind=kOutput, calls=%fused_computation.8.clone.1 | convolution fusion | flops 152223744 | bytes 2953216 | tf_op jit(solution)/shard_map/while/body/eval_jaxpr/dot_general | solution.py:24
  90.9 1.6 %fusion.34 = (f32[384]{0:T(512)S(1)}, f32[384,1536]{1,0:T(8,128)S(1)}) fusion(bf16[8,1536,128]{2,1,0:T(8,128)(2,1)} %get-tuple-element.123, s32[]{:T(128)S(6)} %copy.14, bf16[8,384,128]{2,1,0:T(8,128)(2,1)} %get-tuple-element.122), kind=kOutput, calls=%fused_computation.28.clone.1 | convolution fusion | flops 152174208 | bytes 2853376 | tf_op jit(solution)/shard_map/while/body/eval_jaxpr/dot_general | solution.py:15
  92.5 0.5 fusion.35
  93.0 0.1 dynamic_update_slice.12
  93.1 2.2 %fusion.36 = f32[8,384,128]{2,1,0:T(8,128)} fusion(f32[8,384,128]{2,1,0:T(8,128)} %get-tuple-element.113, s32[]{:T(128)S(6)} %copy.14, f32[384,1536]{1,0:T(8,128)S(1)} %get-tuple-element.100, f32[384]{0:T(512)S(1)} %broadcast_maximum_fusion.2, bf16[8,1536,128]{2,1,0:T(8,128)(2,1)} %get-tuple-element.124, f32[384]{0:T(512)S(1)} %get-tuple-element.102), kind=kOutput, calls=%fused_computation.8.clone.1 | convolution fusion | flops 152223744 | bytes 2953216 | tf_op jit(solution)/shard_map/while/body/eval_jaxpr/dot_general | solution.py:24
  95.3 1.6 %fusion.34 = (f32[384]{0:T(512)S(1)}, f32[384,1536]{1,0:T(8,128)S(1)}) fusion(bf16[8,1536,128]{2,1,0:T(8,128)(2,1)} %get-tuple-element.123, s32[]{:T(128)S(6)} %copy.14, bf16[8,384,128]{2,1,0:T(8,128)(2,1)} %get-tuple-element.122), kind=kOutput, calls=%fused_computation.28.clone.1 | convolution fusion | flops 152174208 | bytes 2853376 | tf_op jit(solution)/shard_map/while/body/eval_jaxpr/dot_general | solution.py:15
  96.9 0.5 fusion.35
  97.4 0.1 dynamic_update_slice.12
  97.4 2.2 %fusion.36 = f32[8,384,128]{2,1,0:T(8,128)} fusion(f32[8,384,128]{2,1,0:T(8,128)} %get-tuple-element.113, s32[]{:T(128)S(6)} %copy.14, f32[384,1536]{1,0:T(8,128)S(1)} %get-tuple-element.100, f32[384]{0:T(512)S(1)} %broadcast_maximum_fusion.2, bf16[8,1536,128]{2,1,0:T(8,128)(2,1)} %get-tuple-element.124, f32[384]{0:T(512)S(1)} %get-tuple-element.102), kind=kOutput, calls=%fused_computation.8.clone.1 | convolution fusion | flops 152223744 | bytes 2953216 | tf_op jit(solution)/shard_map/while/body/eval_jaxpr/dot_general | solution.py:24
  99.6 1.6 %fusion.34 = (f32[384]{0:T(512)S(1)}, f32[384,1536]{1,0:T(8,128)S(1)}) fusion(bf16[8,1536,128]{2,1,0:T(8,128)(2,1)} %get-tuple-element.123, s32[]{:T(128)S(6)} %copy.14, bf16[8,384,128]{2,1,0:T(8,128)(2,1)} %get-tuple-element.122), kind=kOutput, calls=%fused_computation.28.clone.1 | convolution fusion | flops 152174208 | bytes 2853376 | tf_op jit(solution)/shard_map/while/body/eval_jaxpr/dot_general | solution.py:15
  101.2 0.5 fusion.35
  101.7 0.1 dynamic_update_slice.12
  101.8 2.2 %fusion.36 = f32[8,384,128]{2,1,0:T(8,128)} fusion(f32[8,384,128]{2,1,0:T(8,128)} %get-tuple-element.113, s32[]{:T(128)S(6)} %copy.14, f32[384,1536]{1,0:T(8,128)S(1)} %get-tuple-element.100, f32[384]{0:T(512)S(1)} %broadcast_maximum_fusion.2, bf16[8,1536,128]{2,1,0:T(8,128)(2,1)} %get-tuple-element.124, f32[384]{0:T(512)S(1)} %get-tuple-element.102), kind=kOutput, calls=%fused_computation.8.clone.1 | convolution fusion | flops 152223744 | bytes 2953216 | tf_op jit(solution)/shard_map/while/body/eval_jaxpr/dot_general | solution.py:24
  104.0 1.6 %fusion.34 = (f32[384]{0:T(512)S(1)}, f32[384,1536]{1,0:T(8,128)S(1)}) fusion(bf16[8,1536,128]{2,1,0:T(8,128)(2,1)} %get-tuple-element.123, s32[]{:T(128)S(6)} %copy.14, bf16[8,384,128]{2,1,0:T(8,128)(2,1)} %get-tuple-element.122), kind=kOutput, calls=%fused_computation.28.clone.1 | convolution fusion | flops 152174208 | bytes 2853376 | tf_op jit(solution)/shard_map/while/body/eval_jaxpr/dot_general | solution.py:15
  105.6 0.5 fusion.35
  106.1 0.1 dynamic_update_slice.12
  106.2 2.2 %fusion.36 = f32[8,384,128]{2,1,0:T(8,128)} fusion(f32[8,384,128]{2,1,0:T(8,128)} %get-tuple-element.113, s32[]{:T(128)S(6)} %copy.14, f32[384,1536]{1,0:T(8,128)S(1)} %get-tuple-element.100, f32[384]{0:T(512)S(1)} %broadcast_maximum_fusion.2, bf16[8,1536,128]{2,1,0:T(8,128)(2,1)} %get-tuple-element.124, f32[384]{0:T(512)S(1)} %get-tuple-element.102), kind=kOutput, calls=%fused_computation.8.clone.1 | convolution fusion | flops 152223744 | bytes 2953216 | tf_op jit(solution)/shard_map/while/body/eval_jaxpr/dot_general | solution.py:24
  108.4 1.6 %fusion.34 = (f32[384]{0:T(512)S(1)}, f32[384,1536]{1,0:T(8,128)S(1)}) fusion(bf16[8,1536,128]{2,1,0:T(8,128)(2,1)} %get-tuple-element.123, s32[]{:T(128)S(6)} %copy.14, bf16[8,384,128]{2,1,0:T(8,128)(2,1)} %get-tuple-element.122), kind=kOutput, calls=%fused_computation.28.clone.1 | convolution fusion | flops 152174208 | bytes 2853376 | tf_op jit(solution)/shard_map/while/body/eval_jaxpr/dot_general | solution.py:15
  110.0 0.5 fusion.35
  110.5 0.1 dynamic_update_slice.12
  110.5 2.2 %fusion.36 = f32[8,384,128]{2,1,0:T(8,128)} fusion(f32[8,384,128]{2,1,0:T(8,128)} %get-tuple-element.113, s32[]{:T(128)S(6)} %copy.14, f32[384,1536]{1,0:T(8,128)S(1)} %get-tuple-element.100, f32[384]{0:T(512)S(1)} %broadcast_maximum_fusion.2, bf16[8,1536,128]{2,1,0:T(8,128)(2,1)} %get-tuple-element.124, f32[384]{0:T(512)S(1)} %get-tuple-element.102), kind=kOutput, calls=%fused_computation.8.clone.1 | convolution fusion | flops 152223744 | bytes 2953216 | tf_op jit(solution)/shard_map/while/body/eval_jaxpr/dot_general | solution.py:24
  112.7 0.0 copy-start
  112.8 5.2 %multiply_reduce_fusion = (f32[384]{0:T(512)S(1)}, f32[384,2048]{1,0:T(8,128)S(1)}) fusion(bf16[8,128,2048]{2,1,0:T(8,128)(2,1)} %param.14, f32[8,384,128]{2,1,0:T(8,128)} %get-tuple-element.38, f32[8,384]{1,0:T(8,128)S(1)} %get-tuple-element.39, bf16[384,2048]{1,0:T(8,128)(2,1)} %param.9), kind=kOutput, calls=%fused_computation.22 | convolution fusion | flops 1614544512 | bytes 10499584 | tf_op jit(solution)/shard_map/hqd,hde->qe/dot_general | solution.py:61
  118.0 0.0 copy-done
  118.0 1.7 %fusion.23 = bf16[384,2048]{1,0:T(8,128)(2,1)} fusion(bf16[384,2048]{1,0:T(8,128)(2,1)S(1)} %copy-done, f32[384,2048]{1,0:T(8,128)S(1)} %get-tuple-element.57, f32[2048]{0:T(1024)S(1)} %convert_element_type.17, f32[384]{0:T(512)S(1)} %add_rsqrt_fusion, pred[384]{0:T(512)(128)(4,1)S(1)} %broadcast_compare_fusion), kind=kLoop, calls=%fused_computation.23 | loop fusion | flops 3145728 | bytes 6301568 | tf_op jit(solution)/shard_map/jit(_where)/select_n | solution.py:69
  (29 shorter events, 0.2 us)
Async XLA Ops:
  6.5 71.3 %all-gather.2.cloned.1.call-start = ((), (), s32[]{:S(2)}) async-start(), calls=%async_computation.1 | async-start | bytes 3932160 | tf_op jit(solution)/shard_map/all_gather | solution.py:49
  10.8 5.3 %copy-start.1 = (bf16[2048]{0:T(1024)(128)(2,1)S(1)}, bf16[2048]{0:T(1024)(128)(2,1)}, u32[]{:S(2)}) copy-start(bf16[2048]{0:T(1024)(128)(2,1)} %param.15) | copy-start | bytes 12292
  10.8 5.3 %copy-start.2 = (s32[384]{0:T(512)S(1)}, s32[384]{0:T(512)}, u32[]{:S(2)}) copy-start(s32[384]{0:T(512)} %param.13) | copy-start | bytes 4612
  10.8 50.3 %all-to-all-start = ((bf16[4,8,384,128]{3,2,1,0:T(8,128)(2,1)}), bf16[4,8,384,128]{3,2,1,0:T(8,128)(2,1)S(1)}, u32[]{:S(2)}, u32[]{:S(2)}) async-start(bf16[4,8,384,128]{3,2,1,0:T(8,128)(2,1)} %stack.2), calls=%async_computation | async-start | bytes 6291456 | tf_op jit(solution)/shard_map/all_to_all | solution.py:47
  112.7 5.2 %copy-start = (bf16[384,2048]{1,0:T(8,128)(2,1)S(1)}, bf16[384,2048]{1,0:T(8,128)(2,1)}, u32[]{:S(2)}) copy-start(bf16[384,2048]{1,0:T(8,128)(2,1)} %param.9) | copy-start | bytes 4718596
Sparse Core Ops, SparseCore 0:
  9.2 68.5 all-gather.1
